TPU v7x, 32 devices: a whole 2x2x4 slice. The times are simulated.
32 devices in a mesh: gx: 4 (over x, core), gy: 4 (over z), gz: 2 (over y).
Axes of the slice: x: 2, y: 2, z: 4, core: 2. Of those that a mesh axis runs over, the one named last changes fastest.
Arguments:
- features: float32 [64, 64, 64, 128], P('gx', 'gy', 'gz'), may hold values from -6 to 6
- scales: float32 [64, 64, 64], P('gx', 'gy', 'gz'), may hold values from 0.2 to 0.4
- thetas: float32 [2, 4, 128], replicated, may hold values from -1 to 1
- weights: float32 [2, 128, 128], replicated, may hold values from -0.5 to 0.5
Outputs:
- hidden: float32 [64, 64, 64, 128], P('gx', 'gy', 'gz')
All inputs are finite; a program needn't handle non-finite values.
Results may differ from a plain program's by a relative error of at most 0.00011.
Values sent between devices are 32-bit elements; how exact they have to be, the bound alone decides.
A program may use at most 64 MiB of HBM per device.

v0:
```python
import functools

import jax
import jax.numpy as jnp
import numpy as np
from jax import lax
from jax.experimental import pallas as pl
from jax.experimental.pallas import tpu as pltpu
from jax.sharding import PartitionSpec as P

MESH = pl.DeviceIdType.MESH
PLANE_GROUPS = 4


def power_coefficients(order):
    table = np.zeros((order + 1, order + 1))
    table[0, 0] = 1.0
    if order > 0:
        table[1, 1] = 1.0
    for k in range(2, order + 1):
        table[k, 1:] = 2.0 * table[k - 1, :-1]
        table[k] -= table[k - 2]
    return table


def split_weights(w):
    high = w.astype(jnp.bfloat16)
    low = (w - high.astype(jnp.float32)).astype(jnp.bfloat16)
    top = jnp.concatenate([high, low], axis=1)
    bottom = jnp.concatenate([high, jnp.zeros_like(low)], axis=1)
    return jnp.concatenate([top, bottom], axis=0)


def silu(v):
    return v / (1.0 + jnp.exp(-v))


def product(total, packed):
    c = total.shape[-1]
    high = total.astype(jnp.bfloat16)
    low = (total - high.astype(jnp.float32)).astype(jnp.bfloat16)
    out = jnp.dot(
        jnp.concatenate([high, low], axis=1), packed, preferred_element_type=jnp.float32
    )
    return out[:, :c] + out[:, c:]


def diffuse_kernel(
    sizes, features, scales_in, thetas_in, weights_in, out,
    scales, thetas, weights, h, sb, q, zs, zh, wp, tt, in_sem, send_sem, recv_sem,
):
    (nx, ny, nz, c), layers, order = sizes
    table = power_coefficients(order)
    position = {a: lax.axis_index(a) for a in ("gx", "gy", "gz")}

    def near(axis, step):
        size = lax.axis_size(axis)
        return {axis: lax.rem(position[axis] + step + size, size)}

    inner = nx - 2
    cuts = [1 + (inner * g) // PLANE_GROUPS for g in range(PLANE_GROUPS + 1)]
    groups = [(cuts[g], cuts[g + 1]) for g in range(PLANE_GROUPS)]
    faces, middle = (0, ny - 1), tuple(range(1, ny - 1))

    pieces = [(slice(0, nx), y, y + 1) for y in faces]
    pieces += [(slice(a, b), 1, ny - 1) for a, b in [(0, 1), (nx - 1, nx)] + groups]
    loads = []
    for i, (xs, a, b) in enumerate(pieces):
        part = (pl.ds(xs.start, xs.stop - xs.start), pl.ds(a, b - a))
        loads.append(pltpu.make_async_copy(features.at[part], h.at[part], in_sem.at[i]))
    small = [
        pltpu.make_async_copy(src, dst, in_sem.at[len(loads) + i])
        for i, (src, dst) in enumerate(
            [(scales_in, scales), (thetas_in, thetas), (weights_in, weights)]
        )
    ]
    for load in small[:2] + loads + small[2:]:
        load.start()

    barrier = pltpu.get_barrier_semaphore()
    for axis in ("gx", "gy", "gz"):
        for step in (-1, 1):
            pl.semaphore_signal(barrier, inc=1, device_id=near(axis, step), device_id_type=MESH)

    pl.semaphore_wait(barrier, 6)

    def messages(round_index):
        p = round_index % 2
        made = {}

        def add(key, src, dst, axis, step):
            m = len(made)
            made[key] = pltpu.make_async_remote_copy(
                src_ref=src, dst_ref=dst, send_sem=send_sem.at[p, m], recv_sem=recv_sem.at[p, m],
                device_id=near(axis, step), device_id_type=MESH,
            )

        ys = pl.ds(1, ny)
        pair = pl.ds(0, 2)
        for e, x in enumerate((1, nx)):
            add(("ye", 0, e), q.at[p, x, 1], q.at[p, x, ny + 1], "gy", -1)
            add(("ye", 1, e), q.at[p, x, ny], q.at[p, x, 0], "gy", 1)
        add(("x", 0), q.at[p, 1, ys], q.at[p, nx + 1, ys], "gx", -1)
        add(("x", 1), q.at[p, nx, ys], q.at[p, 0, ys], "gx", 1)
        for side in (0, 1):
            add(("ze", side), zs.at[p, side, pair], zh.at[p, 1 - side, pair], "gz", 2 * side - 1)
        for g, (a, b) in enumerate(groups):
            xs = pl.ds(1 + a, b - a)
            add(("y", 0, g), q.at[p, xs, 1], q.at[p, xs, ny + 1], "gy", -1)
            add(("y", 1, g), q.at[p, xs, ny], q.at[p, xs, 0], "gy", 1)
            zx = pl.ds(1 + a, b - a)
            for side in (0, 1):
                add(
                    ("z", side, g), zs.at[p, side, zx], zh.at[p, 1 - side, zx], "gz", 2 * side - 1,
                )
        return made

    def coefficient(layer, k):
        total = None
        for t in range(order + 1):
            if table[t, k] != 0.0:
                term = float(table[t, k]) * thetas[layer, pl.ds(t, 1), :]
                total = term if total is None else total + term
        return total

    sublane = lax.broadcasted_iota(jnp.int32, (nz, c), 0)

    def neighbours(p, x, xo, y):
        v = q[p, x + 1, y + 1]
        below = jnp.where(sublane == 0, zh[p, 0, xo, pl.ds(y, 1), :], pltpu.roll(v, 1, 0))
        above = jnp.where(sublane == nz - 1, zh[p, 1, xo, pl.ds(y, 1), :], pltpu.roll(v, nz - 1, 0))
        return (
            (q[p, x, y + 1] + q[p, x + 2, y + 1])
            + (q[p, x + 1, y] + q[p, x + 1, y + 2])
            + (below + above)
        )

    def put(p, x, xo, y, value):
        q[p, x + 1, y + 1] = value
        zs[p, 0, xo, pl.ds(y, 1), :] = value[0:1]
        zs[p, 1, xo, pl.ds(y, 1), :] = value[nz - 1 : nz]

    stages = layers * order + 1

    def compute(stage, x, xo, ys):
        layer, k = divmod(stage, order)
        p_in, p_out = (stage - 1) % 2, stage % 2
        if stage == 0:
            lead = coefficient(0, order)
            for a, b in ((y, y + 1) for y in ys) if len(ys) == 2 else ((ys[0], ys[-1] + 1),):
                sb[x, a:b] = jnp.broadcast_to(scales[x, a:b][:, :, None], (b - a, nz, c))
            for y in ys:
                put(p_out, x, xo, y, sb[x, y] * (lead * h[x, y]))
        elif k != 0:
            ck = coefficient(layer, order - k)
            for y in ys:
                s = sb[x, y]
                put(p_out, x, xo, y, s * (ck * h[x, y] - s * neighbours(p_in, x, xo, y)))
        else:
            c0 = coefficient(layer - 1, 0)
            for i, y in enumerate(ys):
                tt[pl.ds(i * nz, nz)] = c0 * h[x, y] - sb[x, y] * neighbours(p_in, x, xo, y)
            mixed = product(tt[0 : len(ys) * nz], wp[layer - 1])
            mixed = silu(mixed)
            if stage == stages - 1:
                for i, y in enumerate(ys):
                    out[x, y] = mixed[i * nz : (i + 1) * nz]
            else:
                lead = coefficient(layer, order)
                for i, y in enumerate(ys):
                    value = mixed[i * nz : (i + 1) * nz]
                    h[x, y] = value
                    put(p_out, x, xo, y, sb[x, y] * (lead * value))

    def edge_part(stage, ys):
        @pl.loop(0, 2)
        def _(e):
            compute(stage, e * (nx - 1), e, ys)

    def group_part(stage, g, ys):
        @pl.loop(*groups[g])
        def _(x):
            compute(stage, x, x + 1, ys)

    plan = [
        (
            edge_part,
            [("ye", side, e) for side in (0, 1) for e in (0, 1)],
            [("x", 0), ("x", 1), ("ze", 0), ("ze", 1)],
        )
    ]
    for g in range(PLANE_GROUPS):
        plan.append(
            (
                functools.partial(lambda g, stage, ys: group_part(stage, g, ys), g),
                [("y", side, g) for side in (0, 1)],
                [("z", side, g) for side in (0, 1)],
            )
        )

    history = {}
    for stage in range(stages):
        if stage >= 2:
            for copy in history[stage - 2].values():
                copy.wait_send()
        if stage == stages - 1:
            for part, _, others in plan:
                for key in others:
                    history[stage - 1][key].wait_recv()
                part(stage, middle)
            for part, along, _ in plan:
                for key in along:
                    history[stage - 1][key].wait_recv()
                part(stage, faces)
            continue
        now = history[stage] = messages(stage)
        if stage == 1:
            small[2].wait()
            for layer in range(layers):
                wp[layer] = split_weights(weights[layer])
        if stage == 0:
            small[0].wait()
            small[1].wait()
            loads[0].wait()
            loads[1].wait()
            for part, along, _ in plan:
                part(stage, faces)
                for key in along:
                    now[key].start()
        for i, (part, along, others) in enumerate(plan):
            if stage == 0:
                for load in loads[2:4] if i == 0 else loads[3 + i : 4 + i]:
                    load.wait()
            else:
                for key in others + along:
                    history[stage - 1][key].wait_recv()
                part(stage, faces)
                for key in along:
                    now[key].start()
            part(stage, middle)
            for key in others:
                now[key].start()
    for copy in history[stages - 2].values():
        copy.wait_send()


def per_device(features, scales, thetas, weights):
    nx, ny, nz, c = features.shape
    layers, order = weights.shape[0], thetas.shape[1] - 1
    count = 8 + 4 * PLANE_GROUPS
    f32 = jnp.float32
    hbm = pl.BlockSpec(memory_space=pl.ANY)
    return pl.pallas_call(
        functools.partial(diffuse_kernel, ((nx, ny, nz, c), layers, order)),
        out_shape=pltpu.VMEM(features.shape, f32),
        in_specs=[hbm] * 4,
        out_specs=pl.BlockSpec(memory_space=pltpu.VMEM),
        scratch_shapes=[
            pltpu.VMEM(scales.shape, f32),
            pltpu.VMEM(thetas.shape, f32),
            pltpu.VMEM(weights.shape, f32),
            pltpu.VMEM((nx, ny, nz, c), f32),
            pltpu.VMEM((nx, ny, nz, c), f32),
            pltpu.VMEM((2, nx + 2, ny + 2, nz, c), f32),
            pltpu.VMEM((2, 2, nx, ny, c), f32),
            pltpu.VMEM((2, 2, nx, ny, c), f32),
            pltpu.VMEM((layers, 2 * c, 2 * c), jnp.bfloat16),
            pltpu.VMEM((ny * nz, c), f32),
            pltpu.SemaphoreType.DMA((PLANE_GROUPS + 7,)),
            pltpu.SemaphoreType.DMA((2, count)),
            pltpu.SemaphoreType.DMA((2, count)),
        ],
        compiler_params=pltpu.CompilerParams(
            collective_id=0, has_side_effects=True, vmem_limit_bytes=62_783_488
        ),
        name="diffuse",
    )(features, scales, thetas, weights)


def solution(mesh):
    return jax.shard_map(
        per_device,
        mesh=mesh,
        in_specs=(P("gx", "gy", "gz", None), P("gx", "gy", "gz"), P(), P()),
        out_specs=P("gx", "gy", "gz", None),
        check_vma=False,
    )
```

profile of v0, /device:TPU:1, one launch (start us, length us, event | category | flops | bytes accessed | tf_op | source)
XLA Modules:
  0.0 77.8 jit_solution(301572091042343416)
XLA Ops:
  0.0 75.8 %diffuse.1 = f32[16,16,32,128]{3,2,1,0:T(8,128)S(1)} custom-call(f32[16,16,32,128]{3,2,1,0:T(8,128)} %features.1, f32[16,16,32]{2,1,0:T(8,128)} %scales_in.1, f32[2,4,128]{2,1,0:T(4,128)} %thetas_in.1, f32[2,128,128]{2,1,0:T(8,128)} %weights_in.1), custom_call_target="tpu_custom_call" | custom-call | tf_op jit(solution)/shard_map/diffuse/pallas_call | solution.py:253
  75.8 2.0 %copy.6 = f32[16,16,32,128]{3,2,1,0:T(8,128)} copy(f32[16,16,32,128]{3,2,1,0:T(8,128)S(1)} %diffuse.1) | data formatting | bytes 8388608
where the time goes:
time: 79 us; the launch traced here: 77.8 us
  Pallas kernels  75.8 us (96%)
  local copies, waits for them, and re-layouts  2.02 us (3%)
    pallas_call x1, Pallas kernels, per_device(): pl.pallas_call(functools.partial(diffuse_kernel, ((nx, ny, nz, c), layers...  75.8 us
    unnamed x1, local copies, waits for them, and re-layouts  2.02 us

commit v1 on v0

--- a/solution.py
+++ b/solution.py
@@ -9,7 +9,9 @@
 from jax.sharding import PartitionSpec as P
 
 MESH = pl.DeviceIdType.MESH
+AXES = ("gx", "gy", "gz")
 PLANE_GROUPS = 4
+HELD = 2
 
 
 def power_coefficients(order):
@@ -47,15 +49,19 @@
 
 def diffuse_kernel(
     sizes, features, scales_in, thetas_in, weights_in, out,
-    scales, thetas, weights, h, sb, q, zs, zh, wp, tt, in_sem, send_sem, recv_sem,
+    scales, thetas, weights, h, sb, q, zs, zh, wp, tt, in_sem, send_sem, recv_sem, ready,
 ):
     (nx, ny, nz, c), layers, order = sizes
     table = power_coefficients(order)
-    position = {a: lax.axis_index(a) for a in ("gx", "gy", "gz")}
+    position = {a: lax.axis_index(a) for a in AXES}
 
     def near(axis, step):
         size = lax.axis_size(axis)
         return {axis: lax.rem(position[axis] + step + size, size)}
+
+    def leads(axis, side):
+        last = lax.axis_size(axis) - 1
+        return jnp.where(side == 1, position[axis] == last, position[axis] > 0)
 
     inner = nx - 2
     cuts = [1 + (inner * g) // PLANE_GROUPS for g in range(PLANE_GROUPS + 1)]
@@ -74,45 +80,71 @@
             [(scales_in, scales), (thetas_in, thetas), (weights_in, weights)]
         )
     ]
+    barrier = pltpu.get_barrier_semaphore()
+    for axis in AXES:
+        for side in (0, 1):
+            @pl.when(jnp.logical_not(leads(axis, side)))
+            def _():
+                pl.semaphore_signal(
+                    barrier, inc=1, device_id=near(axis, 2 * side - 1), device_id_type=MESH
+                )
     for load in small[:2] + loads + small[2:]:
         load.start()
-
-    barrier = pltpu.get_barrier_semaphore()
-    for axis in ("gx", "gy", "gz"):
-        for step in (-1, 1):
-            pl.semaphore_signal(barrier, inc=1, device_id=near(axis, step), device_id_type=MESH)
-
-    pl.semaphore_wait(barrier, 6)
+    leaders = sum(leads(axis, side).astype(jnp.int32) for axis in AXES for side in (0, 1))
+
+    @pl.when(leaders > 0)
+    def _():
+        pl.semaphore_wait(barrier, leaders)
+
+    for a, axis in enumerate(AXES):
+        for side in (0, 1):
+            @pl.when(leads(axis, side))
+            def _():
+                pl.semaphore_signal(
+                    ready.at[a, 1 - side], inc=1, device_id=near(axis, 2 * side - 1),
+                    device_id_type=MESH,
+                )
+
+    def meet(a, side):
+        @pl.when(jnp.logical_not(leads(AXES[a], side)))
+        def _():
+            pl.semaphore_wait(ready.at[a, side], 1)
+
+    gy_last = lax.axis_size("gy") - 1
+    outer = jnp.logical_or(position["gy"] == 0, position["gy"] == gy_last)
+    first = outer.astype(jnp.int32)
 
     def messages(round_index):
         p = round_index % 2
         made = {}
 
-        def add(key, src, dst, axis, step):
-            m = len(made)
+        def add(key, src, dst, axis, side, m=None):
+            m = len(made) if m is None else m
             made[key] = pltpu.make_async_remote_copy(
                 src_ref=src, dst_ref=dst, send_sem=send_sem.at[p, m], recv_sem=recv_sem.at[p, m],
-                device_id=near(axis, step), device_id_type=MESH,
+                device_id=near(axis, 2 * side - 1), device_id_type=MESH,
             )
+
+        def along(key, xs):
+            m = len(made)
+            for turn in (0, 1):
+                side = first if turn == 0 else 1 - first
+                src, dst = 1 + side * (ny - 1), (1 - side) * (ny + 1)
+                add(key + (turn,), q.at[p, xs, src], q.at[p, xs, dst], "gy", side, m + side)
 
         ys = pl.ds(1, ny)
         pair = pl.ds(0, 2)
         for e, x in enumerate((1, nx)):
-            add(("ye", 0, e), q.at[p, x, 1], q.at[p, x, ny + 1], "gy", -1)
-            add(("ye", 1, e), q.at[p, x, ny], q.at[p, x, 0], "gy", 1)
-        add(("x", 0), q.at[p, 1, ys], q.at[p, nx + 1, ys], "gx", -1)
+            along(("ye", e), x)
+        add(("x", 0), q.at[p, 1, ys], q.at[p, nx + 1, ys], "gx", 0)
         add(("x", 1), q.at[p, nx, ys], q.at[p, 0, ys], "gx", 1)
         for side in (0, 1):
-            add(("ze", side), zs.at[p, side, pair], zh.at[p, 1 - side, pair], "gz", 2 * side - 1)
+            add(("ze", side), zs.at[p, side, pair], zh.at[p, 1 - side, pair], "gz", side)
         for g, (a, b) in enumerate(groups):
             xs = pl.ds(1 + a, b - a)
-            add(("y", 0, g), q.at[p, xs, 1], q.at[p, xs, ny + 1], "gy", -1)
-            add(("y", 1, g), q.at[p, xs, ny], q.at[p, xs, 0], "gy", 1)
-            zx = pl.ds(1 + a, b - a)
+            along(("y", g), xs)
             for side in (0, 1):
-                add(
-                    ("z", side, g), zs.at[p, side, zx], zh.at[p, 1 - side, zx], "gz", 2 * side - 1,
-                )
+                add(("z", side, g), zs.at[p, side, xs], zh.at[p, 1 - side, xs], "gz", side)
         return made
 
     def coefficient(layer, k):
@@ -185,7 +217,7 @@
     plan = [
         (
             edge_part,
-            [("ye", side, e) for side in (0, 1) for e in (0, 1)],
+            [("ye", e, turn) for turn in (0, 1) for e in (0, 1)],
             [("x", 0), ("x", 1), ("ze", 0), ("ze", 1)],
         )
     ]
@@ -193,12 +225,13 @@
         plan.append(
             (
                 functools.partial(lambda g, stage, ys: group_part(stage, g, ys), g),
-                [("y", side, g) for side in (0, 1)],
+                [("y", g, turn) for turn in (0, 1)],
                 [("z", side, g) for side in (0, 1)],
             )
         )
 
     history = {}
+    held = []
     for stage in range(stages):
         if stage >= 2:
             for copy in history[stage - 2].values():
@@ -223,10 +256,18 @@
             small[1].wait()
             loads[0].wait()
             loads[1].wait()
-            for part, along, _ in plan:
+            for i, (part, along, _) in enumerate(plan):
                 part(stage, faces)
+                if i == 0:
+                    meet(1, first)
                 for key in along:
-                    now[key].start()
+                    if key[-1] == 0:
+                        now[key].start()
+            meet(1, 1 - first)
+            for _, along, _ in plan:
+                for key in along:
+                    if key[-1] == 1:
+                        now[key].start()
         for i, (part, along, others) in enumerate(plan):
             if stage == 0:
                 for load in loads[2:4] if i == 0 else loads[3 + i : 4 + i]:
@@ -236,8 +277,16 @@
                     history[stage - 1][key].wait_recv()
                 part(stage, faces)
                 for key in along:
-                    now[key].start()
+                    if key[-1] == 0:
+                        now[key].start()
+                held += [now[key] for key in along if key[-1] == 1]
+                while len(held) > (0 if i == len(plan) - 1 else HELD):
+                    held.pop(0).start()
             part(stage, middle)
+            if stage == 0 and i == 0:
+                for a in (0, 2):
+                    for side in (0, 1):
+                        meet(a, side)
             for key in others:
                 now[key].start()
     for copy in history[stages - 2].values():
@@ -269,6 +318,7 @@
             pltpu.SemaphoreType.DMA((PLANE_GROUPS + 7,)),
             pltpu.SemaphoreType.DMA((2, count)),
             pltpu.SemaphoreType.DMA((2, count)),
+            pltpu.SemaphoreType.REGULAR((3, 2)),
         ],
         compiler_params=pltpu.CompilerParams(
             collective_id=0, has_side_effects=True, vmem_limit_bytes=62_783_488

time: 79 us -> 76.3 us (0.966)
  Pallas kernels: 75.8 us -> 72.9 us
    pallas_call x1, Pallas kernels: 75.8 us -> 72.9 us  [per_device(): pl.pallas_call(functools.partial(diffuse_kernel, ((nx, ny, nz, c), layers...]
where the time goes in v1:
time: 76.3 us; the launch traced here: 75 us
  Pallas kernels  72.9 us (96%)
  local copies, waits for them, and re-layouts  2.02 us (3%)
    pallas_call x1, Pallas kernels, per_device(): pl.pallas_call(functools.partial(diffuse_kernel, ((nx, ny, nz, c), layers...  72.9 us
    unnamed x1, local copies, waits for them, and re-layouts  2.02 us

profile of v1, /device:TPU:1, one launch (start us, length us, event | category | flops | bytes accessed | tf_op | source)
XLA Modules:
  0.0 75.0 jit_solution(14853760079862599519)
XLA Ops:
  0.0 72.9 %diffuse.1 = f32[16,16,32,128]{3,2,1,0:T(8,128)S(1)} custom-call(f32[16,16,32,128]{3,2,1,0:T(8,128)} %features.1, f32[16,16,32]{2,1,0:T(8,128)} %scales_in.1, f32[2,4,128]{2,1,0:T(4,128)} %thetas_in.1, f32[2,128,128]{2,1,0:T(8,128)} %weights_in.1), custom_call_target="tpu_custom_call" | custom-call | tf_op jit(solution)/shard_map/diffuse/pallas_call | solution.py:302
  72.9 2.0 %copy.6 = f32[16,16,32,128]{3,2,1,0:T(8,128)} copy(f32[16,16,32,128]{3,2,1,0:T(8,128)S(1)} %diffuse.1) | data formatting | bytes 8388608

commit v2 on v1

--- a/solution.py
+++ b/solution.py
@@ -10,8 +10,10 @@
 
 MESH = pl.DeviceIdType.MESH
 AXES = ("gx", "gy", "gz")
-PLANE_GROUPS = 4
-HELD = 2
+PLANE_SHARES = (0, 5, 9, 12, 14)
+PLANE_GROUPS = len(PLANE_SHARES) - 1
+ORDERLY = 2
+HOLD = 2
 
 
 def power_coefficients(order):
@@ -64,7 +66,7 @@
         return jnp.where(side == 1, position[axis] == last, position[axis] > 0)
 
     inner = nx - 2
-    cuts = [1 + (inner * g) // PLANE_GROUPS for g in range(PLANE_GROUPS + 1)]
+    cuts = [1 + (inner * share) // PLANE_SHARES[-1] for share in PLANE_SHARES]
     groups = [(cuts[g], cuts[g + 1]) for g in range(PLANE_GROUPS)]
     faces, middle = (0, ny - 1), tuple(range(1, ny - 1))
 
@@ -231,7 +233,30 @@
         )
 
     history = {}
-    held = []
+    held, lagged = [], []
+    slow = lax.rem(position['gx'], 2) == 1
+
+    def dispatch(copies, wait, queue, limit):
+        if wait is None:
+            for copy in copies:
+                copy.start()
+            return
+
+        @pl.when(jnp.logical_not(wait))
+        def _():
+            for copy in copies:
+                copy.start()
+
+        queue += copies
+        ready_now = []
+        while len(queue) > limit:
+            ready_now.append(queue.pop(0))
+        if ready_now:
+            @pl.when(wait)
+            def _():
+                for copy in ready_now:
+                    copy.start()
+
     for stage in range(stages):
         if stage >= 2:
             for copy in history[stage - 2].values():
@@ -276,12 +301,12 @@
                 for key in others + along:
                     history[stage - 1][key].wait_recv()
                 part(stage, faces)
-                for key in along:
-                    if key[-1] == 0:
-                        now[key].start()
-                held += [now[key] for key in along if key[-1] == 1]
-                while len(held) > (0 if i == len(plan) - 1 else HELD):
-                    held.pop(0).start()
+                ahead, behind = (
+                    [now[key] for key in along if key[-1] == turn] for turn in (0, 1)
+                )
+                final = i == len(plan) - 1
+                dispatch(ahead, slow if stage >= ORDERLY else None, lagged, 0 if final else HOLD)
+                dispatch(behind, outer, held, 0 if final else HOLD)
             part(stage, middle)
             if stage == 0 and i == 0:
                 for a in (0, 2):

time: 76.3 us -> 75.5 us (0.990); the launches traced: 75 us -> 75.3 us
  no operation moved by 1% of the time
where the time goes in v2:
time: 75.5 us; the launch traced here: 75.3 us
  Pallas kernels  73.3 us (97%)
  local copies, waits for them, and re-layouts  2.02 us (3%)
    pallas_call x1, Pallas kernels, per_device(): pl.pallas_call(functools.partial(diffuse_kernel, ((nx, ny, nz, c), layers...  73.3 us
    unnamed x1, local copies, waits for them, and re-layouts  2.02 us

profile of v2, /device:TPU:1, one launch (start us, length us, event | category | flops | bytes accessed | tf_op | source)
XLA Modules:
  0.0 75.3 jit_solution(5572927397516048296)
XLA Ops:
  0.0 73.3 %diffuse.1 = f32[16,16,32,128]{3,2,1,0:T(8,128)S(1)} custom-call(f32[16,16,32,128]{3,2,1,0:T(8,128)} %features.1, f32[16,16,32]{2,1,0:T(8,128)} %scales_in.1, f32[2,4,128]{2,1,0:T(4,128)} %thetas_in.1, f32[2,128,128]{2,1,0:T(8,128)} %weights_in.1), custom_call_target="tpu_custom_call" | custom-call | tf_op jit(solution)/shard_map/diffuse/pallas_call | solution.py:327
  73.3 2.0 %copy.6 = f32[16,16,32,128]{3,2,1,0:T(8,128)} copy(f32[16,16,32,128]{3,2,1,0:T(8,128)S(1)} %diffuse.1) | data formatting | bytes 8388608

commit v3 on v2

--- a/solution.py
+++ b/solution.py
@@ -90,7 +90,7 @@
                 pl.semaphore_signal(
                     barrier, inc=1, device_id=near(axis, 2 * side - 1), device_id_type=MESH
                 )
-    for load in small[:2] + loads + small[2:]:
+    for load in small[:2] + loads[:2]:
         load.start()
     leaders = sum(leads(axis, side).astype(jnp.int32) for axis in AXES for side in (0, 1))
 
@@ -106,6 +106,9 @@
                     ready.at[a, 1 - side], inc=1, device_id=near(axis, 2 * side - 1),
                     device_id_type=MESH,
                 )
+
+    for load in loads[2:] + small[2:]:
+        load.start()
 
     def meet(a, side):
         @pl.when(jnp.logical_not(leads(AXES[a], side)))

time: 75.5 us -> 75.5 us (level)
  no operation moved by 1% of the time
where the time goes in v3:
time: 75.5 us; the launch traced here: 75.3 us
  Pallas kernels  73.3 us (97%)
  local copies, waits for them, and re-layouts  2.02 us (3%)
    pallas_call x1, Pallas kernels, per_device(): pl.pallas_call(functools.partial(diffuse_kernel, ((nx, ny, nz, c), layers...  73.3 us
    unnamed x1, local copies, waits for them, and re-layouts  2.02 us

profile of v3, /device:TPU:1, one launch (start us, length us, event | category | flops | bytes accessed | tf_op | source)
XLA Modules:
  0.0 75.3 jit_solution(2118304260985211230)
XLA Ops:
  0.0 73.3 %diffuse.1 = f32[16,16,32,128]{3,2,1,0:T(8,128)S(1)} custom-call(f32[16,16,32,128]{3,2,1,0:T(8,128)} %features.1, f32[16,16,32]{2,1,0:T(8,128)} %scales_in.1, f32[2,4,128]{2,1,0:T(4,128)} %thetas_in.1, f32[2,128,128]{2,1,0:T(8,128)} %weights_in.1), custom_call_target="tpu_custom_call" | custom-call | tf_op jit(solution)/shard_map/diffuse/pallas_call | solution.py:330
  73.3 2.0 %copy.6 = f32[16,16,32,128]{3,2,1,0:T(8,128)} copy(f32[16,16,32,128]{3,2,1,0:T(8,128)S(1)} %diffuse.1) | data formatting | bytes 8388608
